TPU v7x, 256 devices: a 8x8x2 block of a 8x8x16 slice. The times are simulated.
256 devices in a mesh: groups: 2 (over z), attn: 16 (over y, core), expert: 8 (over x).
Axes of the slice: x: 8, y: 8, z: 2, core: 2. Of those that a mesh axis runs over, the one named last changes fastest.
The devices are a block of a 8x8x16 slice.
Arguments:
- tokens: bfloat16 [4096, 4096], P(('groups', 'attn'), 'expert'), parts along dimension 0, may hold values from -6 to 6
- expert_ids: int32 [4096, 8], P(('groups', 'attn')), parts along dimension 0, may hold values from 0 to 63, all different within a row; in each aligned block of 128 rows (0 to 127, 128 to 255, ...) at most 48 rows name the same one
- gate_weight: bfloat16 [4096, 8], P(('groups', 'attn')), parts along dimension 0, may hold values from 0.049804688 to 0.29882812
- w_gate: bfloat16 [64, 4096, 768], P('attn', 'expert'), may hold values from -0.09375 to 0.09375
- w_up: bfloat16 [64, 4096, 768], P('attn', 'expert'), may hold values from -0.09375 to 0.09375
- w_down: bfloat16 [64, 768, 4096], P('attn', None, 'expert'), may hold values from -0.21875 to 0.21875
- query: bfloat16 [512, 64, 128], P(('groups', 'attn', 'expert')), parts along dimension 0, may hold values from -100 to 100
- cache_k: bfloat16 [512, 768, 4, 128], P(('groups', 'attn', 'expert')), parts along dimension 0, may hold values from -6 to 6
- cache_v: bfloat16 [512, 768, 4, 128], P(('groups', 'attn', 'expert')), parts along dimension 0, may hold values from -6 to 6
- lengths: int32 [512], P(('groups', 'attn', 'expert')), parts along dimension 0, may hold values from 2 to 768, as said below
Outputs:
- moe_out: bfloat16 [4096, 4096], P(('groups', 'attn'), 'expert'), parts along dimension 0
- attn_out: bfloat16 [512, 8192], P(('groups', 'attn', 'expert')), parts along dimension 0
There are 2 independent parts, one for each index of `groups`. A program takes and returns all parts, laid end to end along the dimension named above; an argument that names none is the same for every part. Nothing has to cross between parts.
Inputs may be any that keep to these rules, and one draw needn't show every extreme that they name: `expert_ids`: each row names 8 different experts. In the rows of one index of attn (aligned blocks of 128 rows) no expert is named by more than 48 rows, and in some block some expert by exactly 48. `lengths`: some sequence has all 768 positions live.
All inputs are finite; a program needn't handle non-finite values.
Results may differ from a plain program's by a relative error of at most 0.025.
Values may be sent and summed in bfloat16 or wider, within the bound.
A program may use at most 64 MiB of HBM per device.

v0:
```python
import jax
import jax.numpy as jnp
from jax import lax
from jax.sharding import PartitionSpec as P


def laid_out(tiles, dim):
    dims = list(tiles.shape[1:])
    dims[dim] *= tiles.shape[0]
    return jnp.moveaxis(tiles, 0, dim).reshape(dims)


def copy_for_each(shard, axis):
    count = lax.axis_size(axis)
    return lax.all_to_all(
        jnp.broadcast_to(shard[None], (count, *shard.shape)), axis, 0, 0, tiled=True
    )


def gather_directly(shard, axis, dim):
    return laid_out(copy_for_each(shard, axis), dim)


def member_table(expert_ids, experts):
    wanted = jnp.arange(experts, dtype=jnp.int32)
    return jnp.any(expert_ids[:, :, None] == wanted[None, None, :], axis=1).astype(jnp.int32)


def pad_rows(values):
    feat_width = values.shape[-1]
    flat_rows = values.reshape(-1, feat_width)
    return jnp.concatenate([flat_rows, jnp.zeros((1, feat_width), values.dtype)], axis=0)


def return_slots(results, starts_in, kept_in, slot_count):
    local_experts = results.shape[0]
    capacity = results.shape[1]
    slot_ids = jnp.arange(slot_count, dtype=jnp.int32)[None, None, :]
    column = jnp.arange(local_experts, dtype=jnp.int32)[None, :, None]
    row_index = column * capacity + starts_in[:, :, None] + slot_ids
    row_index = jnp.where(slot_ids < kept_in[:, :, None], row_index, local_experts * capacity)
    return pad_rows(results)[row_index]


def grouped_attention(query, cache_k, cache_v, lengths):
    seq_count, head_total, head_size = query.shape
    context = cache_k.shape[1]
    kv_count = cache_k.shape[2]
    grouped = query.reshape(seq_count, kv_count, head_total // kv_count, head_size)
    scores = jnp.einsum(
        "skgd,slkd->skgl", grouped, cache_k, preferred_element_type=jnp.float32
    ) * head_size ** (-0.5)
    live_mask = (
        lax.broadcasted_iota(jnp.int32, (seq_count, 1, 1, context), 3)
        < lengths[:, None, None, None]
    )
    masked = jnp.where(live_mask, scores, -jnp.inf)
    row_peak = jnp.max(masked, axis=3, keepdims=True)
    weighted = jnp.exp(masked - row_peak)
    denominator = jnp.sum(weighted, axis=3, keepdims=True)
    prob_bf = (weighted / denominator).astype(jnp.bfloat16)
    attended = jnp.einsum("skgl,slkd->skgd", prob_bf, cache_v, preferred_element_type=jnp.float32)
    return attended.reshape(seq_count, head_total * head_size).astype(jnp.bfloat16)


def body(tokens, expert_ids, gate_weight, w_gate, w_up, w_down, query, cache_k, cache_v, lengths):
    tok_rows, feat_width = tokens.shape
    top_count = expert_ids.shape[1]
    local_experts = w_gate.shape[0]
    ffn_width = w_gate.shape[2]
    attn_count = lax.axis_size("attn")
    experts = local_experts * attn_count
    capacity = tok_rows * top_count // local_experts
    slot_count = min(tok_rows, 3 * tok_rows * top_count // experts)
    member = member_table(expert_ids, experts)
    local_rank = jnp.cumsum(member, axis=0, dtype=jnp.int32) - member
    whole_ids = None
    whole_tokens, whole_ids, whole_gates = (
        gather_directly(tokens, "attn", 0),
        gather_directly(expert_ids, "attn", 0),
        gather_directly(gate_weight, "attn", 0),
    )
    all_rows = whole_tokens.shape[0]
    whole_member = member_table(whole_ids, experts)
    all_counts = jnp.sum(
        whole_member.reshape(attn_count, tok_rows, experts), axis=1, dtype=jnp.int32
    )
    src_offsets = jnp.cumsum(all_counts, axis=0, dtype=jnp.int32) - all_counts
    src_kept = jnp.clip(capacity - src_offsets, 0, all_counts)
    my_index = lax.axis_index("attn")
    offsets = lax.dynamic_index_in_dim(src_offsets, my_index, 0, keepdims=False)
    position = offsets[None, :] + local_rank
    starts_in = lax.dynamic_slice_in_dim(src_offsets, my_index * local_experts, local_experts, 1)
    kept_in = lax.dynamic_slice_in_dim(src_kept, my_index * local_experts, local_experts, 1)
    my_member = lax.dynamic_slice_in_dim(whole_member, my_index * local_experts, local_experts, 1)
    queue_place = jnp.cumsum(my_member, axis=0, dtype=jnp.int32) - my_member
    pack_target = jnp.where(
        (my_member > 0) & (queue_place < capacity),
        jnp.arange(local_experts, dtype=jnp.int32)[None, :] * capacity + queue_place,
        local_experts * capacity,
    )
    holders = jnp.broadcast_to(
        jnp.arange(all_rows, dtype=jnp.int32)[:, None], (all_rows, local_experts)
    )
    pack_index = (
        jnp.full((local_experts * capacity,), all_rows, jnp.int32)
        .at[pack_target.reshape(-1)]
        .set(holders.reshape(-1), mode="drop")
    )
    packed = pad_rows(whole_tokens)[pack_index].reshape(local_experts, capacity, feat_width)
    gate_part = jnp.einsum("jrd,jdf->jrf", packed, w_gate, preferred_element_type=jnp.float32)
    up_part = jnp.einsum("jrd,jdf->jrf", packed, w_up, preferred_element_type=jnp.float32)
    both_parts = jnp.concatenate([gate_part, up_part], axis=2)
    row_sums = lax.psum_scatter(
        both_parts.astype(jnp.bfloat16), "expert", scatter_dimension=1, tiled=True
    ).astype(jnp.float32)
    hidden_share = (jax.nn.silu(row_sums[:, :, :ffn_width]) * row_sums[:, :, ffn_width:]).astype(
        jnp.bfloat16
    )
    hidden = gather_directly(hidden_share, "expert", 1)
    results = jnp.einsum("jrf,jfd->jrd", hidden, w_down, preferred_element_type=jnp.float32).astype(
        jnp.bfloat16
    )
    back_rows = return_slots(results, starts_in, kept_in, slot_count)
    returned = lax.all_to_all(back_rows, "attn", split_axis=0, concat_axis=0, tiled=True)
    slot_of = jnp.take_along_axis(local_rank, expert_ids, axis=1)
    place_of = jnp.take_along_axis(position, expert_ids, axis=1)
    keep_mask = place_of < capacity
    picked = returned.reshape(experts * slot_count, feat_width)[expert_ids * slot_count + slot_of]
    factor = jnp.where(keep_mask, gate_weight.astype(jnp.float32), 0.0)
    moe_out = jnp.sum(factor[:, :, None] * picked.astype(jnp.float32), axis=1).astype(jnp.bfloat16)
    attn_out = grouped_attention(query, cache_k, cache_v, lengths)
    return (moe_out, attn_out)


def solution(mesh):
    return jax.shard_map(
        body,
        mesh=mesh,
        in_specs=(
            P(("groups", "attn"), "expert"),
            P(("groups", "attn"), None),
            P(("groups", "attn"), None),
            P("attn", "expert", None),
            P("attn", "expert", None),
            P("attn", None, "expert"),
            P(("groups", "attn", "expert"), None, None),
            P(("groups", "attn", "expert"), None, None, None),
            P(("groups", "attn", "expert"), None, None, None),
            P(("groups", "attn", "expert")),
        ),
        out_specs=(P(("groups", "attn"), "expert"), P(("groups", "attn", "expert"), None)),
        check_vma=False,
    )
```

profile of v0, /device:TPU:513, one launch (start us, length us, event | category | flops | bytes accessed | tf_op | source)
XLA Modules:
  0.0 318.8 jit_solution(7994495979518382753)
XLA Ops:
  8.0 30.9 %all_to_all.20 = s32[16,128,8]{1,2,0:T(8,128)S(1)} all-to-all(s32[16,128,8]{1,2,0:T(8,128)S(1)} %broadcast_in_dim.36), channel_id=1, replica_groups=mesh['groups'=2,'attn'=16,'expert'=8] {'attn'}, dimensions={0} | all-to-all | bytes 131072 | tf_op jit(solution)/shard_map/all_to_all | solution.py:15
  38.9 2.5 broadcast_in_dim.39
  41.4 4.5 %all-to-all-start.1 = ((bf16[16,128,512]{2,1,0:T(8,128)(2,1)}), bf16[16,128,512]{2,1,0:T(8,128)(2,1)}, u32[]{:S(2)}, u32[]{:S(2)}) async-start(bf16[16,128,512]{2,1,0:T(8,128)(2,1)} %broadcast_in_dim.39), calls=%async_computation.1 | async-start | bytes 4194304 | tf_op jit(solution)/shard_map/all_to_all | solution.py:15
  47.0 1.8 reshape.197
  51.2 1.2 reduce-window.6
  53.8 1.3 copy.130
  55.2 2.0 reshape.148
  57.2 30.4 %scatter_custom_fusion = s32[1024]{0:T(1024)S(1)} fusion(s32[8192]{0:T(1024)S(1)} %bitcast.73, s32[8192]{0:T(1024)S(1)} %reshape.197, s32[]{:T(128)} %constant.35.clone.1), kind=kCustom, calls=%fused_computation.58 | custom fusion | bytes 4100 | tf_op jit(solution)/shard_map/scatter | solution.py:108
  87.6 7.5 %all-to-all-done.1 = bf16[16,128,512]{2,1,0:T(8,128)(2,1)} async-done(((bf16[16,128,512]{2,1,0:T(8,128)(2,1)}), bf16[16,128,512]{2,1,0:T(8,128)(2,1)}, u32[]{:S(2)}, u32[]{:S(2)}) %all-to-all-start.1) | async-done | bytes 2097184 | tf_op jit(solution)/shard_map/all_to_all | solution.py:15
  95.2 3.1 concatenate.10
  98.3 7.0 %gather_fusion = bf16[1024,512]{1,0:T(8,128)(2,1)} fusion(bf16[2049,512]{1,0:T(8,128)(2,1)} %concatenate.10, s32[1024]{0:T(1024)S(1)} %fusion.22), kind=kCustom, calls=%fused_computation.2 | custom fusion | bytes 2101248 | tf_op jit(solution)/shard_map/gather | solution.py:110
  105.3 2.4 convolution_convert_fusion
  108.8 1.9 pad_maximum_fusion
  110.8 45.1 %reduce-scatter.2.cloned.1.call-done = bf16[4,32,1536]{2,1,0:T(8,128)(2,1)} async-done(((bf16[4,256,1536]{2,1,0:T(8,128)(2,1)}), bf16[4,32,1536]{2,1,0:T(8,128)(2,1)}) %reduce-scatter.2.cloned.1.call-update) | async-done | bytes 393232 | tf_op jit(solution)/shard_map/reduce_scatter | solution.py:114
  155.9 1.1 convert_element_type.45
  157.1 1.3 broadcast_in_dim.48
  158.4 5.5 %all-to-all-start.2 = ((bf16[8,4,32,768]{3,2,1,0:T(8,128)(2,1)}), bf16[8,4,32,768]{3,2,1,0:T(8,128)(2,1)}, u32[]{:S(2)}, u32[]{:S(2)}) async-start(bf16[8,4,32,768]{3,2,1,0:T(8,128)(2,1)} %broadcast_in_dim.48), calls=%async_computation.3 | async-start | bytes 3145728 | tf_op jit(solution)/shard_map/all_to_all | solution.py:15
  164.0 1.9 copy.138
  165.9 2.2 reduce_sum.27
  168.5 33.4 %all-to-all-done.2 = bf16[8,4,32,768]{3,2,1,0:T(8,128)(2,1)} async-done(((bf16[8,4,32,768]{3,2,1,0:T(8,128)(2,1)}), bf16[8,4,32,768]{3,2,1,0:T(8,128)(2,1)}, u32[]{:S(2)}, u32[]{:S(2)}) %all-to-all-start.2) | async-done | bytes 1572896 | tf_op jit(solution)/shard_map/all_to_all | solution.py:15
  201.9 1.7 copy.131
  205.2 1.1 concatenate.12
  206.3 14.7 %gather_fusion.1 = bf16[3072,512]{1,0:T(8,128)(2,1)} fusion(bf16[1025,512]{1,0:T(8,128)(2,1)} %concatenate.12, s32[3072]{0:T(1024)S(1)} %broadcast_clamp_fusion), kind=kCustom, calls=%fused_computation.3 | custom fusion | bytes 6303744 | tf_op jit(solution)/shard_map/gather | solution.py:42
  221.0 9.9 %all-to-all-start.3 = ((bf16[16,4,48,512]{3,2,1,0:T(8,128)(2,1)}), bf16[16,4,48,512]{3,2,1,0:T(8,128)(2,1)}, u32[]{:S(2)}, u32[]{:S(2)}) async-start(bf16[16,4,48,512]{3,2,1,0:T(8,128)(2,1)} %bitcast.65), calls=%async_computation.4 | async-start | bytes 6291456 | tf_op jit(solution)/shard_map/all_to_all | solution.py:125
  232.1 1.9 fusion.12
  234.9 2.5 fusion.15
  237.4 1.4 copy.157
  239.6 7.1 %gather_fusion.3 = s32[1024]{0:T(1024)S(1)} fusion(s32[128,64]{1,0:T(8,128)S(1)} %get-tuple-element.3, s32[1024]{0:T(1024)S(1)} %reshape.217), kind=kCustom, calls=%fused_computation.clone | custom fusion | bytes 16384 | tf_op jit(solution)/shard_map/jit(take_along_axis)/gather | solution.py:127
  246.7 7.1 %gather_fusion.4 = s32[1024]{0:T(1024)S(1)} fusion(s32[128,64]{1,0:T(8,128)S(1)} %get-tuple-element.4, s32[1024]{0:T(1024)S(1)} %reshape.217), kind=kCustom, calls=%fused_computation.1.clone | custom fusion | bytes 16384 | tf_op jit(solution)/shard_map/jit(take_along_axis)/gather | solution.py:126
  254.5 47.5 %all-to-all-done.3 = bf16[16,4,48,512]{3,2,1,0:T(8,128)(2,1)} async-done(((bf16[16,4,48,512]{3,2,1,0:T(8,128)(2,1)}), bf16[16,4,48,512]{3,2,1,0:T(8,128)(2,1)}, u32[]{:S(2)}, u32[]{:S(2)}) %all-to-all-start.3) | async-done | bytes 3145760 | tf_op jit(solution)/shard_map/all_to_all | solution.py:125
  301.9 7.4 %gather_fusion.2 = bf16[1024,512]{1,0:T(8,128)(2,1)} fusion(bf16[3072,512]{1,0:T(8,128)(2,1)} %bitcast.12, s32[1024]{0:T(1024)S(1)} %broadcast_clamp_fusion.1), kind=kCustom, calls=%fused_computation.4 | custom fusion | bytes 2101248 | tf_op jit(solution)/shard_map/gather | solution.py:129
  309.3 2.6 fusion.2
  (64 shorter events, 12.7 us)
Async XLA Ops:
  7.2 98.1 %copy-start = (bf16[4,512,768]{2,1,0:T(8,128)(2,1)S(1)}, bf16[4,512,768]{2,1,0:T(8,128)(2,1)}, u32[]{:S(2)}) copy-start(bf16[4,512,768]{2,1,0:T(8,128)(2,1)} %param.16) | copy-start | bytes 9437188
  41.4 53.8 %all-to-all-start.1 = ((bf16[16,128,512]{2,1,0:T(8,128)(2,1)}), bf16[16,128,512]{2,1,0:T(8,128)(2,1)}, u32[]{:S(2)}, u32[]{:S(2)}) async-start(bf16[16,128,512]{2,1,0:T(8,128)(2,1)} %broadcast_in_dim.39), calls=%async_computation.1 | async-start | bytes 4194304 | tf_op jit(solution)/shard_map/all_to_all | solution.py:15
  45.9 110.0 %reduce-scatter.2.cloned.1.call-start = ((), (), s32[]{:S(2)}) async-start(), calls=%async_computation.5 | async-start | bytes 3538944 | tf_op jit(solution)/shard_map/reduce_scatter | solution.py:114
  50.4 0.8 copy-start.3
  105.3 2.4 copy-start.1
  105.3 2.5 copy-start.2
  158.4 43.5 %all-to-all-start.2 = ((bf16[8,4,32,768]{3,2,1,0:T(8,128)(2,1)}), bf16[8,4,32,768]{3,2,1,0:T(8,128)(2,1)}, u32[]{:S(2)}, u32[]{:S(2)}) async-start(bf16[8,4,32,768]{3,2,1,0:T(8,128)(2,1)} %broadcast_in_dim.48), calls=%async_computation.3 | async-start | bytes 3145728 | tf_op jit(solution)/shard_map/all_to_all | solution.py:15
  201.9 2.4 copy-start.8
  221.0 9.9 %copy-start.5 = (s32[128,8]{0,1:T(8,128)S(1)}, s32[128,8]{0,1:T(8,128)}, u32[]{:S(2)}) copy-start(s32[128,8]{0,1:T(8,128)} %param.13) | copy-start | bytes 12292
  221.0 11.1 %copy-start.7 = (s32[2]{0:T(128)S(1)}, s32[2]{0:T(128)}, u32[]{:S(2)}) copy-start(s32[2]{0:T(128)} %param.21) | copy-start | bytes 28
  221.0 80.9 %all-to-all-start.3 = ((bf16[16,4,48,512]{3,2,1,0:T(8,128)(2,1)}), bf16[16,4,48,512]{3,2,1,0:T(8,128)(2,1)}, u32[]{:S(2)}, u32[]{:S(2)}) async-start(bf16[16,4,48,512]{3,2,1,0:T(8,128)(2,1)} %bitcast.65), calls=%async_computation.4 | async-start | bytes 6291456 | tf_op jit(solution)/shard_map/all_to_all | solution.py:125
  231.0 1.1 copy-start.4
  246.7 7.6 %copy-start.6 = (bf16[128,8]{0,1:T(8,128)(2,1)S(1)}, bf16[128,8]{0,1:T(8,128)(2,1)}, u32[]{:S(2)}) copy-start(bf16[128,8]{0,1:T(8,128)(2,1)} %param.14) | copy-start | bytes 6148
Sparse Core Ops, SparseCore 0:
  110.9 44.9 reduce-scatter.1
where the time goes:
time: 320 us; the launch traced here: 319 us
  waiting for transfers between devices  134 us (42%)
  local copies, waits for them, and re-layouts  96.5 us (30%)
  blocking collectives  30.9 us (10%)
  starting transfers between devices  20 us (6%)
  other arithmetic  14.7 us (5%)
  between operations  14.3 us (4%)
  matrix products  8.71 us (3%)
    all_to_all x1, waiting for transfers between devices, body(): lax.all_to_all(back_rows, 'attn', split_axis=0, concat_axis=0, tiled=True)  47.5 us
    reduce_scatter x1, waiting for transfers between devices, body(): lax.psum_scatter(both_parts.astype(jnp.bfloat16), 'expert', scatter_dimen...  45.1 us
    all_to_all x2, waiting for transfers between devices, copy_for_each(): lax.all_to_all(jnp.broadcast_to(shard[None], (count, *shard.shape)), axis...  40.9 us
    all_to_all x1, blocking collectives, copy_for_each(): lax.all_to_all(jnp.broadcast_to(shard[None], (count, *shard.shape)), axis...  30.9 us
    scatter x1, local copies, waits for them, and re-layouts, body(): pack_index = jnp.full((local_experts * capacity,), all_rows, jnp.int32).a...  30.4 us
    gather x1, local copies, waits for them, and re-layouts, return_slots(): return pad_rows(results)[row_index]  14.7 us
    all_to_all x2, starting transfers between devices, copy_for_each(): lax.all_to_all(jnp.broadcast_to(shard[None], (count, *shard.shape)), axis...  10.1 us
    all_to_all x1, starting transfers between devices, body(): lax.all_to_all(back_rows, 'attn', split_axis=0, concat_axis=0, tiled=True)  9.88 us
  transfers between devices with their start and end apart: 4, of which 4 were waited for; matrix products, arithmetic and copies ran while one was open for 22% of the time, Pallas kernels for 0%

commit v1 on v0

v1 whole, which is shorter than its diff:
```python
import jax
import jax.numpy as jnp
from jax import lax
from jax.sharding import PartitionSpec as P


def grouped_attention(query, cache_k, cache_v, lengths):
    seq_count, head_total, head_size = query.shape
    context = cache_k.shape[1]
    kv_count = cache_k.shape[2]
    grouped = query.reshape(seq_count, kv_count, head_total // kv_count, head_size)
    scores = jnp.einsum(
        "skgd,slkd->skgl", grouped, cache_k, preferred_element_type=jnp.float32
    ) * head_size ** (-0.5)
    live_mask = (
        lax.broadcasted_iota(jnp.int32, (seq_count, 1, 1, context), 3)
        < lengths[:, None, None, None]
    )
    masked = jnp.where(live_mask, scores, -jnp.inf)
    row_peak = jnp.max(masked, axis=3, keepdims=True)
    weighted = jnp.exp(masked - row_peak)
    denominator = jnp.sum(weighted, axis=3, keepdims=True)
    prob_bf = (weighted / denominator).astype(jnp.bfloat16)
    attended = jnp.einsum("skgl,slkd->skgd", prob_bf, cache_v, preferred_element_type=jnp.float32)
    return attended.reshape(seq_count, head_total * head_size).astype(jnp.bfloat16)


def body(tokens, expert_ids, gate_weight, w_gate, w_up, w_down, query, cache_k, cache_v, lengths):
    tok_rows, feat_width = tokens.shape
    top_count = expert_ids.shape[1]
    local_experts = w_gate.shape[0]
    ffn_width = w_gate.shape[2]
    attn_count = lax.axis_size("attn")
    capacity = tok_rows * top_count // local_experts
    extra = tok_rows * top_count // feat_width
    block = jnp.concatenate(
        [
            tokens,
            expert_ids.astype(jnp.bfloat16).reshape(extra, feat_width),
            gate_weight.reshape(extra, feat_width),
        ],
        axis=0,
    )
    whole = lax.all_gather(block, "attn", axis=0, tiled=False)
    whole_tokens = whole[:, :tok_rows].reshape(attn_count * tok_rows, feat_width)
    whole_ids = whole[:, tok_rows : tok_rows + extra].reshape(attn_count * tok_rows, top_count)
    whole_gates = whole[:, tok_rows + extra :].reshape(attn_count * tok_rows, top_count)
    mine = lax.axis_index("attn") * local_experts + jnp.arange(local_experts, dtype=jnp.int32)
    equal = whole_ids.astype(jnp.int32)[:, :, None] == mine[None, None, :]
    member = jnp.any(equal, axis=1).astype(jnp.int32)
    gates = jnp.sum(jnp.where(equal, whole_gates.astype(jnp.float32)[:, :, None], 0.0), axis=1)
    place = jnp.where(member > 0, jnp.cumsum(member, axis=0, dtype=jnp.int32) - member, -1)
    slots = jnp.arange(capacity, dtype=jnp.int32)
    pick = (place.T[:, None, :] == slots[None, :, None]).astype(jnp.bfloat16)
    packed = jnp.einsum("jrt,td->jrd", pick, whole_tokens, preferred_element_type=jnp.float32).astype(
        jnp.bfloat16
    )
    gate_part = jnp.einsum("jrd,jdf->jrf", packed, w_gate, preferred_element_type=jnp.float32)
    up_part = jnp.einsum("jrd,jdf->jrf", packed, w_up, preferred_element_type=jnp.float32)
    both_parts = jnp.concatenate([gate_part, up_part], axis=2)
    row_sums = lax.psum_scatter(
        both_parts.astype(jnp.bfloat16), "expert", scatter_dimension=1, tiled=True
    ).astype(jnp.float32)
    hidden_share = (jax.nn.silu(row_sums[:, :, :ffn_width]) * row_sums[:, :, ffn_width:]).astype(
        jnp.bfloat16
    )
    hidden = lax.all_gather(hidden_share, "expert", axis=1, tiled=True)
    results = jnp.einsum("jrf,jfd->jrd", hidden, w_down, preferred_element_type=jnp.float32).astype(
        jnp.bfloat16
    )
    weigh = jnp.where(place[:, :, None] == slots[None, None, :], gates[:, :, None], 0.0).astype(
        jnp.bfloat16
    )
    partial = jnp.einsum("tjr,jrd->td", weigh, results, preferred_element_type=jnp.float32)
    moe_out = lax.psum_scatter(
        partial.astype(jnp.bfloat16), "attn", scatter_dimension=0, tiled=True
    )
    attn_out = grouped_attention(query, cache_k, cache_v, lengths)
    return (moe_out, attn_out)


def solution(mesh):
    return jax.shard_map(
        body,
        mesh=mesh,
        in_specs=(
            P(("groups", "attn"), "expert"),
            P(("groups", "attn"), None),
            P(("groups", "attn"), None),
            P("attn", "expert", None),
            P("attn", "expert", None),
            P("attn", None, "expert"),
            P(("groups", "attn", "expert"), None, None),
            P(("groups", "attn", "expert"), None, None, None),
            P(("groups", "attn", "expert"), None, None, None),
            P(("groups", "attn", "expert")),
        ),
        out_specs=(P(("groups", "attn"), "expert"), P(("groups", "attn", "expert"), None)),
        check_vma=False,
    )
```

time: 320 us -> 248 us (0.78)
  local copies, waits for them, and re-layouts: 96.5 us -> 11.5 us
  waiting for transfers between devices: 134 us -> 196 us
  blocking collectives: 30.9 us -> 0 us
  starting transfers between devices: 20 us -> 0.26 us
  matrix products: 8.71 us -> 14.6 us
  other arithmetic: 14.7 us -> 9.26 us
    all_gather x0 -> x2, waiting for transfers between devices: none -> 96.5 us  [the longest x1 60 us: body(): whole = lax.all_gather(block, 'attn', axis=0, tiled=False)]
    all_to_all x3 -> x0, waiting for transfers between devices: 88.4 us -> none  [the longest x1 47.5 us: body(): lax.all_to_all(back_rows, 'attn', split_axis=0, concat_axis=0, tiled=True)]
    reduce_scatter x0 -> x1, waiting for transfers between devices: none -> 56.3 us  [body(): lax.psum_scatter(partial.astype(jnp.bfloat16), 'attn', scatter_dimension=...]
    gather x11 -> x0, local copies, waits for them, and re-layouts: 43.7 us -> none  [the longest x1 14.7 us: return_slots(): return pad_rows(results)[row_index]]
    all_to_all x1 -> x0, blocking collectives: 30.9 us -> none  [copy_for_each(): lax.all_to_all(jnp.broadcast_to(shard[None], (count, *shard.shape)), axis...]
    scatter x1 -> x0, local copies, waits for them, and re-layouts: 30.4 us -> none  [body(): pack_index = jnp.full((local_experts * capacity,), all_rows, jnp.int32).a...]
    all_to_all x3 -> x0, starting transfers between devices: 20 us -> none  [the longest x2 10.1 us: copy_for_each(): lax.all_to_all(jnp.broadcast_to(shard[None], (count, *shard.shape)), axis...]
    dot_general x1 -> x2, matrix products: 0.97 us -> 8.25 us  [the longest x1 5.92 us: body(): jnp.einsum('tjr,jrd->td', weigh, results, preferred_element_type=jnp.floa...]
  transfers between devices with their start and end apart: 4 -> 4, of which waited for: 4 -> 4; matrix products, arithmetic and copies ran while one was open for 22% -> 4% of each run, Pallas kernels for 0% -> 0%
where the time goes in v1:
time: 248 us; the launch traced here: 246 us
  waiting for transfers between devices  196 us (79%)
  matrix products  14.6 us (6%)
  between operations  13.9 us (6%)
  local copies, waits for them, and re-layouts  11.5 us (5%)
  other arithmetic  9.26 us (4%)
    all_gather x1, waiting for transfers between devices, body(): whole = lax.all_gather(block, 'attn', axis=0, tiled=False)  60 us
    reduce_scatter x1, waiting for transfers between devices, body(): lax.psum_scatter(partial.astype(jnp.bfloat16), 'attn', scatter_dimension=...  56.3 us
    reduce_scatter x1, waiting for transfers between devices, body(): lax.psum_scatter(both_parts.astype(jnp.bfloat16), 'expert', scatter_dimen...  43.2 us
    all_gather x1, waiting for transfers between devices, body(): hidden = lax.all_gather(hidden_share, 'expert', axis=1, tiled=True)  36.5 us
    dot_general x1, matrix products, body(): jnp.einsum('tjr,jrd->td', weigh, results, preferred_element_type=jnp.floa...  5.92 us
  transfers between devices with their start and end apart: 4, of which 4 were waited for; matrix products, arithmetic and copies ran while one was open for 4% of the time, Pallas kernels for 0%

profile of v1, /device:TPU:513, one launch (start us, length us, event | category | flops | bytes accessed | tf_op | source)
XLA Modules:
  0.0 245.8 jit_solution(15599072337729525529)
XLA Ops:
  7.3 0.9 copy.23
  8.3 0.7 convert_element_type.62
  9.0 0.1 copy.22
  9.1 0.1 reshape.71
  9.2 1.6 maximum_bitcast_fusion
  11.0 60.0 %all-gather.7.cloned.1.call-done = bf16[16,132,512]{2,1,0:T(8,128)(2,1)} async-done(((bf16[1,132,512]{2,1,0:T(8,128)(2,1)}), bf16[16,132,512]{2,1,0:T(8,128)(2,1)}) %all-gather.7.cloned.1.call-update) | async-done | bytes 2162704 | tf_op jit(solution)/shard_map/all_gather | solution.py:44
  71.0 1.0 slice_convert_fusion.1
  72.1 1.6 reshape.77
  73.6 1.5 copy.24
  75.2 0.2 compare_reduce_fusion
  75.4 1.2 reduce-window.6
  76.5 0.2 slice_reduce_fusion
  76.7 0.2 reduce-window.9
  77.0 1.5 slice-done
  78.5 2.3 fusion.11
  80.9 1.0 convolution_convert_fusion
  81.9 0.9 copy-done.2
  82.8 1.0 convolution_convert_fusion.1
  83.8 1.9 pad_maximum_fusion
  85.8 43.2 %reduce-scatter.3.cloned.1.call-done = bf16[4,32,1536]{2,1,0:T(8,128)(2,1)} async-done(((bf16[4,256,1536]{2,1,0:T(8,128)(2,1)}), bf16[4,32,1536]{2,1,0:T(8,128)(2,1)}) %reduce-scatter.3.cloned.1.call-update) | async-done | bytes 393232 | tf_op jit(solution)/shard_map/reduce_scatter | solution.py:61
  129.0 1.1 convert_element_type.72
  130.1 0.8 fusion.23
  131.0 1.6 reshape.78
  132.6 1.5 copy.25
  134.1 0.2 fusion.24
  134.4 36.5 %all-gather.5.cloned.1.call-done = bf16[4,256,768]{2,1,0:T(8,128)(2,1)} async-done(((bf16[4,32,768]{2,1,0:T(8,128)(2,1)}), bf16[4,256,768]{2,1,0:T(8,128)(2,1)}) %all-gather.5.cloned.1.call-update) | async-done | bytes 1572880 | tf_op jit(solution)/shard_map/all_gather | solution.py:67
  170.8 5.9 %bitcast_convert_fusion = bf16[2048,512]{1,0:T(8,128)(2,1)} fusion(bf16[2048,4]{0,1:T(4,128)(2,1)S(1)} %fusion.24, s32[2048,4]{0,1:T(4,128)S(1)} %fusion.29, bf16[4,256,768]{2,1,0:T(8,128)(2,1)} %all-gather.5.cloned.1.call-done, bf16[4,768,512]{2,1,0:T(8,128)(2,1)S(1)} %copy-done), kind=kOutput, calls=%fused_computation.6 | convolution fusion | flops 2958557184 | bytes 6864896 | tf_op jit(solution)/shard_map/tjr,jrd->td/dot_general | solution.py:74
  176.9 1.9 fusion.17
  178.8 0.2 fusion.32
  179.1 2.4 fusion.20
  181.5 1.4 copy.45
  182.9 56.3 %reduce-scatter.5.cloned.1.call-done = bf16[128,512]{1,0:T(8,128)(2,1)} async-done(((bf16[2048,512]{1,0:T(8,128)(2,1)}), bf16[128,512]{1,0:T(8,128)(2,1)}) %reduce-scatter.5.cloned.1.call-update) | async-done | bytes 131088 | tf_op jit(solution)/shard_map/reduce_scatter | solution.py:75
  (24 shorter events, 0.8 us)
Async XLA Ops:
  7.2 163.6 %copy-start = (bf16[4,768,512]{2,1,0:T(8,128)(2,1)S(1)}, bf16[4,768,512]{2,1,0:T(8,128)(2,1)}, u32[]{:S(2)}) copy-start(bf16[4,768,512]{2,1,0:T(8,128)(2,1)} %param.15) | copy-start | bytes 9437188
  7.2 63.8 %all-gather.7.cloned.1.call-start = ((), (), s32[]{:S(2)}) async-start(), calls=%async_computation.5 | async-start | bytes 2367488 | tf_op jit(solution)/shard_map/all_gather | solution.py:44
  10.9 118.1 %reduce-scatter.3.cloned.1.call-start = ((), (), s32[]{:S(2)}) async-start(), calls=%async_computation.2 | async-start | bytes 3538944 | tf_op jit(solution)/shard_map/reduce_scatter | solution.py:61
  76.9 1.6 slice-start
  78.5 2.3 copy-start.1
  80.9 1.9 copy-start.2
  85.8 85.1 %all-gather.5.cloned.1.call-start = ((), (), s32[]{:S(2)}) async-start(), calls=%async_computation.3 | async-start | bytes 1769472 | tf_op jit(solution)/shard_map/all_gather | solution.py:67
  131.0 108.3 %reduce-scatter.5.cloned.1.call-start = ((), (), s32[]{:S(2)}) async-start(), calls=%async_computation.4 | async-start | bytes 2228224 | tf_op jit(solution)/shard_map/reduce_scatter | solution.py:75
  134.3 42.5 %copy-start.3 = (s32[2]{0:T(128)S(1)}, s32[2]{0:T(128)}, u32[]{:S(2)}) copy-start(s32[2]{0:T(128)} %param.19) | copy-start | bytes 28
Sparse Core Ops, SparseCore 0:
  11.0 59.9 all-gather.6
  85.9 43.1 reduce-scatter.2
  131.1 39.6 all-gather.4
  176.9 62.2 reduce-scatter.4

commit v2 on v1

v2 whole, which is shorter than its diff:
```python
import functools

import jax
import jax.numpy as jnp
from jax import lax
from jax.experimental import pallas as pl
from jax.experimental.pallas import tpu as pltpu
from jax.sharding import PartitionSpec as P

MESH = pl.DeviceIdType.MESH
BF16 = jnp.bfloat16
F32 = jnp.float32
CORES = 2


def dot(a, b):
    return jnp.dot(a, b, preferred_element_type=F32)


def kernel(
    ny, nx, kv_heads,
    ids_ref, gates_ref, tok_ref, len_ref, q_ref, wg_hbm, wu_hbm, wd_hbm, k_hbm, v_hbm,
    moe_ref, attn_ref,
    wgu, wd, kbuf, vbuf, tok_all, info_all, memb_s, gate_s, pos_s, pos_t, gate_t, acc, part, rs_buf,
    hid, out_all, weigh, comb, d2_send, d2_recv, y_send, y_recv,
    load_sem, inf_s, inf_r, infd_s, infd_r, ag_s, ag_r, agd_s, agd_r, rs_s, rs_r, hx_s, hx_r,
    rd_s, rd_r, ry_s, ry_r,
):
    experts, feat, ff = wg_hbm.shape
    rows = tok_ref.shape[0]
    cap = acc.shape[1]
    share = cap // nx
    hy, hx = ny // 2, nx // 2
    blocks = ny * CORES
    ai, xi = lax.axis_index("attn"), lax.axis_index("expert")
    y, c = lax.div(ai, CORES), lax.rem(ai, CORES)

    def ring(i, n):
        return lax.rem(i + n, n)

    def at_y(i):
        return {"attn": ring(i, ny) * CORES + c}

    partner = {"attn": y * CORES + (1 - c)}
    y_dev = (at_y(y + 1), at_y(y - 1))
    x_dev = ({"expert": ring(xi + 1, nx)}, {"expert": ring(xi - 1, nx)})
    sign = (1, -1)
    sent = []

    def send(src, dst, ss, rs, dev):
        copy = pltpu.make_async_remote_copy(
            src_ref=src, dst_ref=dst, send_sem=ss, recv_sem=rs, device_id=dev, device_id_type=MESH
        )
        copy.start()
        sent.append(copy)
        return copy

    loads = [
        pltpu.make_async_copy(k_hbm, kbuf, load_sem.at[0]),
        pltpu.make_async_copy(v_hbm, vbuf, load_sem.at[1]),
        pltpu.make_async_copy(wg_hbm, wgu.at[:, :, pl.ds(0, ff)], load_sem.at[2]),
        pltpu.make_async_copy(wu_hbm, wgu.at[:, :, pl.ds(ff, ff)], load_sem.at[3]),
        pltpu.make_async_copy(wd_hbm, wd, load_sem.at[4]),
    ]
    for load in loads:
        load.start()
    info = jnp.concatenate([ids_ref[...].astype(F32), gates_ref[...].astype(F32)], axis=0).astype(BF16)
    info_all[y, c] = info
    tok_all[y, c] = tok_ref[...]

    barrier = pltpu.get_barrier_semaphore()
    peers = [at_y(y + k) for k in range(1, ny)] + [partner, x_dev[0], x_dev[1]]
    for dev in peers:
        pl.semaphore_signal(barrier, inc=1, device_id=dev, device_id_type=MESH)
    pl.semaphore_wait(barrier, len(peers))

    info_copy = {
        k: send(info_all.at[y, c], info_all.at[y, c], inf_s.at[k - 1], inf_r.at[k - 1], at_y(y + k))
        for k in range(1, ny)
    }
    info_pair = {0: send(info_all.at[y, c], info_all.at[y, c], infd_s.at[0], infd_r.at[0], partner)}
    half = rows // 2

    def tok_view(piece, yo):
        return tok_all.at[yo, c, pl.ds(piece * half, half)]

    def last_piece(d):
        return d

    ag, pair = {}, {}

    def ag_send(piece, d, s):
        yo = ring(y - sign[d] * (s - 1), ny)
        src = tok_ref.at[pl.ds(piece * half, half)] if s == 1 else tok_view(piece, yo)
        ag[piece, d, s] = send(
            src, tok_view(piece, yo), ag_s.at[piece, d, s - 1], ag_r.at[piece, d, s - 1], y_dev[d]
        )

    def pair_send(piece, d, s):
        yo = ring(y - sign[d] * s, ny)
        slot = 0 if s == 0 else 1 + d * hy + s - 1
        src = tok_ref.at[pl.ds(piece * half, half)] if s == 0 else tok_view(piece, yo)
        pair[piece, d, s] = send(
            src, tok_view(piece, yo), agd_s.at[piece, slot], agd_r.at[piece, slot], partner
        )

    for piece in range(2):
        for d in range(2):
            ag_send(piece, d, 1)
    for piece in range(2):
        pair_send(piece, 0, 0)

    def ag_step(s):
        for piece in range(2):
            for d in range(2):
                if s == hy and piece != last_piece(d):
                    continue
                ag[piece, d, s].wait_recv()
                if s + 1 < hy or (s + 1 == hy and piece == last_piece(d)):
                    ag_send(piece, d, s + 1)
                pair_send(piece, d, s)

    def attention(i):
        heads, size = q_ref.shape[1:]
        keys = kbuf.shape[1]
        group = heads // kv_heads
        scores = lax.dot_general(
            q_ref[i], kbuf[i], (((1,), (1,)), ((), ())), preferred_element_type=F32
        ) * size ** (-0.5)
        col = lax.broadcasted_iota(jnp.int32, (heads, keys), 1)
        head = lax.broadcasted_iota(jnp.int32, (heads, keys), 0)
        live = (lax.rem(col, kv_heads) == lax.div(head, group)) & (
            col < len_ref[i] * kv_heads
        )
        masked = jnp.where(live, scores, -jnp.inf)
        weighted = jnp.exp(masked - jnp.max(masked, axis=1, keepdims=True))
        total = jnp.sum(weighted, axis=1, keepdims=True)
        prob = (weighted * (1.0 / total)).astype(BF16)
        attn_ref[i] = dot(prob, vbuf[i]).astype(BF16)

    loads[0].wait()
    loads[1].wait()
    attention(0)
    ag_step(1)
    for k in range(1, ny):
        info_copy[k].wait_recv()
        yo = ring(y - k, ny)
        info_pair[k] = send(
            info_all.at[yo, c], info_all.at[yo, c], infd_s.at[k], infd_r.at[k], partner
        )
    for i in range(1, q_ref.shape[0]):
        attention(i)
    ag_step(2)

    for k in range(ny):
        info_pair[k].wait_recv()
    top = ids_ref.shape[0]
    first = ai * experts
    for b in range(blocks):
        both = info_all[b // CORES, b % CORES].astype(F32)
        for e in range(experts):
            equal = both[:top] == (first + e).astype(F32)
            row = e * blocks + b
            memb_s[row : row + 1, :] = jnp.sum(jnp.where(equal, 1.0, 0.0), axis=0, keepdims=True)
            gate_s[row : row + 1, :] = jnp.sum(jnp.where(equal, both[top:], 0.0), axis=0, keepdims=True)
    lines = experts * blocks
    member = memb_s[...]
    iota0 = lax.broadcasted_iota(jnp.int32, (rows, rows), 0)
    iota1 = lax.broadcasted_iota(jnp.int32, (rows, rows), 1)
    before = dot(member.astype(BF16), jnp.where(iota0 < iota1, 1.0, 0.0).astype(BF16))
    counts = dot(member.astype(BF16), jnp.ones((rows, rows), BF16))
    line0 = lax.broadcasted_iota(jnp.int32, (lines, lines), 0)
    line1 = lax.broadcasted_iota(jnp.int32, (lines, lines), 1)
    earlier = (lax.div(line0, blocks) == lax.div(line1, blocks)) & (line1 < line0)
    offset = dot(jnp.where(earlier, 1.0, 0.0).astype(BF16), counts.astype(BF16))
    place = jnp.where(member > 0.5, before + offset, -1.0)
    pos_s[...] = place
    pad = jnp.zeros((rows - lines, rows), F32)
    pos_t[...] = jnp.concatenate([place, pad], axis=0).T
    gate_t[...] = jnp.concatenate([gate_s[...], pad], axis=0).T

    slot_row = lax.broadcasted_iota(jnp.int32, (cap, rows), 0).astype(F32)

    def dispatch(e, yc):
        picks = []
        for cc in range(CORES):
            line = pos_s[pl.ds(e * blocks + yc * CORES + cc, 1), :]
            picks.append(jnp.where(line == slot_row, 1.0, 0.0))
        pick = jnp.concatenate(picks, axis=1).astype(BF16)
        return dot(pick, tok_all[yc].reshape(CORES * rows, feat))

    def pair_wait(s):
        for (piece, d, at), copy in pair.items():
            if at == s:
                copy.wait_recv()

    pair_wait(0)
    for e in range(experts):
        acc[e] = dispatch(e, y)

    def dispatch_step(s):
        pair_wait(s)
        for d in range(2):
            for e in range(experts):
                acc[e] += dispatch(e, ring(y - sign[d] * s, ny))

    dispatch_step(1)
    for s in range(3, hy + 1):
        ag_step(s)
        dispatch_step(s - 1)
    pair_wait(hy)

    loads[2].wait()
    loads[3].wait()
    rs = {}
    half_share = share // 2

    def rs_send(e, d, s):
        dest = ring(xi + sign[d] * (hx + 1 - s), nx)
        if s == 1:
            at = pl.ds(d * half_share, half_share)
            src, dst = part.at[e, dest, at], rs_buf.at[d, 0, e, at]
        else:
            src, dst = rs_buf.at[d, s - 2, e], rs_buf.at[d, s - 1, e]
        rs[e, d, s] = send(src, dst, rs_s.at[e, d, s - 1], rs_r.at[e, d, s - 1], x_dev[d])

    wide = 2 * ff
    step_cols = wide // 3
    for e in range(experts):
        packed = (acc[e] + dispatch(e, ring(y + hy, ny))).astype(BF16)
        for n in range(3):
            at = pl.ds(n * step_cols, step_cols)
            part[e, :, :, at] = (
                dot(packed, wgu[e, :, at]).astype(BF16).reshape(nx, share, step_cols)
            )
        for d in range(2):
            rs_send(e, d, 1)

    slot_col = lax.broadcasted_iota(jnp.int32, (rows, cap), 1).astype(F32)

    def weigh_block(b):
        for e in range(experts):
            line = e * blocks + b
            at_col = pos_t[:, line : line + 1]
            gate_col = gate_t[:, line : line + 1]
            weigh[b // CORES, b % CORES, :, e * cap : (e + 1) * cap] = jnp.where(
                at_col == slot_col, gate_col, 0.0
            ).astype(BF16)

    todo = list(range(blocks))
    for s in range(1, hx):
        for e in range(experts):
            for d in range(2):
                rs[e, d, s].wait_recv()
                dest = ring(xi + sign[d] * (hx - s), nx)
                if s == 1:
                    got, new = pl.ds(d * half_share, half_share), pl.ds((1 - d) * half_share, half_share)
                    rs_buf[d, 0, e, got] = (
                        rs_buf[d, 0, e, got].astype(F32) + part[e, dest, got].astype(F32)
                    ).astype(BF16)
                    rs_buf[d, 0, e, new] = part[e, dest, new]
                else:
                    rs_buf[d, s - 1, e] = (
                        rs_buf[d, s - 1, e].astype(F32) + part[e, dest].astype(F32)
                    ).astype(BF16)
                rs_send(e, d, s + 1)
            for _ in range(2):
                if todo:
                    weigh_block(todo.pop(0))

    hd = {}

    def hid_send(e, d, s):
        xo = ring(xi - sign[d] * (s - 1), nx)
        view = hid.at[e, xo]
        if s == hx:
            view = hid.at[e, xo, pl.ds(d * half_share, half_share)]
        hd[e, d, s] = send(view, view, hx_s.at[e, d, s - 1], hx_r.at[e, d, s - 1], x_dev[d])

    for e in range(experts):
        for d in range(2):
            rs[e, d, hx].wait_recv()
        total = part[e, xi].astype(F32) + rs_buf[0, hx - 1, e].astype(F32) + rs_buf[1, hx - 1, e].astype(F32)
        gate = total[:, :ff]
        hid[e, xi] = (gate / (1.0 + jnp.exp(-gate)) * total[:, ff:]).astype(BF16)
        for d in range(2):
            hid_send(e, d, 1)
    for s in range(1, hx):
        for e in range(experts):
            for d in range(2):
                hd[e, d, s].wait_recv()
                hid_send(e, d, s + 1)
    loads[4].wait()
    for e in range(experts):
        for d in range(2):
            hd[e, d, hx].wait_recv()
        out_all[e * cap : (e + 1) * cap, :] = dot(hid[e].reshape(cap, ff), wd[e]).astype(BF16)

    def slot_of(d, k):
        return 0 if k == 0 else ny - 1 if k == hy else 2 * k - 1 + d

    rd = {}

    def combine(d, k):
        slot = slot_of(d, k)
        yd = ring(y + sign[d] * k, ny)
        d2_send[slot] = dot(weigh[yd, 1 - c], out_all[...]).astype(BF16)
        rd[slot] = send(d2_send.at[slot], d2_recv.at[slot], rd_s.at[slot], rd_r.at[slot], partner)
        comb[slot] = dot(weigh[yd, c], out_all[...])

    def join(d, k):
        slot = slot_of(d, k)
        rd[slot].wait_recv()
        comb[slot] += d2_recv[slot].astype(F32)

    pieces = 4
    tall = rows // pieces
    ry = {}

    def ry_has(p, d, s):
        return s > 1 or (p >= pieces // 2) == (d == 1)

    def ry_step(s):
        for p in range(pieces):
            for d in range(2):
                if not ry_has(p, d, s):
                    continue
                at = pl.ds(p * tall, tall)
                value = comb[slot_of(d, hy + 1 - s), at]
                if s > 1 and ry_has(p, d, s - 1):
                    ry[p, d, s - 1].wait_recv()
                    value = value + y_recv[d, s - 2, at].astype(F32)
                y_send[d, s - 1, at] = value.astype(BF16)
                ry[p, d, s] = send(
                    y_send.at[d, s - 1, at], y_recv.at[d, s - 1, at],
                    ry_s.at[p, d, s - 1], ry_r.at[p, d, s - 1], y_dev[d],
                )

    combine(0, hy)
    for s in range(1, hy + 1):
        k = hy - s
        for d in range(2 if k else 1):
            combine(d, k)
        for d in range(2 if s > 1 else 1):
            join(d, k + 1)
        ry_step(s)
    join(0, 0)
    for p in range(pieces):
        at = pl.ds(p * tall, tall)
        value = comb[0, at]
        for d in range(2):
            ry[p, d, hy].wait_recv()
            value = value + y_recv[d, hy - 1, at].astype(F32)
        moe_ref[at, :] = value.astype(BF16)
    for copy in sent:
        copy.wait_send()


def body(tokens, expert_ids, gate_weight, w_gate, w_up, w_down, query, cache_k, cache_v, lengths):
    rows, feat = tokens.shape
    top = expert_ids.shape[1]
    experts, _, ff = w_gate.shape
    attn, nx = lax.axis_size("attn"), lax.axis_size("expert")
    ny = attn // CORES
    cap = rows * top // experts
    share = cap // nx
    seqs, heads, size = query.shape
    context, kv_heads = cache_k.shape[1:3]
    keys = context * kv_heads
    lines = experts * attn
    hy, hx = ny // 2, nx // 2
    vmem = pltpu.VMEM
    sem = pltpu.SemaphoreType.DMA
    in_vmem = pl.BlockSpec(memory_space=vmem)
    in_hbm = pl.BlockSpec(memory_space=pl.ANY)
    moe, attended = pl.pallas_call(
        functools.partial(kernel, ny, nx, kv_heads),
        out_shape=(
            jax.ShapeDtypeStruct((rows, feat), BF16),
            jax.ShapeDtypeStruct((seqs, heads, size), BF16),
        ),
        in_specs=[in_vmem, in_vmem, in_vmem, pl.BlockSpec(memory_space=pltpu.SMEM), in_vmem] + [in_hbm] * 5,
        out_specs=(in_vmem, in_vmem),
        scratch_shapes=[
            vmem((experts, feat, 2 * ff), BF16),
            vmem((experts, ff, feat), BF16),
            vmem((seqs, keys, size), BF16),
            vmem((seqs, keys, size), BF16),
            vmem((ny, CORES, rows, feat), BF16),
            vmem((ny, CORES, 2 * top, rows), BF16),
            vmem((lines, rows), F32),
            vmem((lines, rows), F32),
            vmem((lines, rows), F32),
            vmem((rows, rows), F32),
            vmem((rows, rows), F32),
            vmem((experts, cap, feat), F32),
            vmem((experts, nx, share, 2 * ff), BF16),
            vmem((2, hx, experts, share, 2 * ff), BF16),
            vmem((experts, nx, share, ff), BF16),
            vmem((experts * cap, feat), BF16),
            vmem((ny, CORES, rows, experts * cap), BF16),
            vmem((ny, rows, feat), F32),
            vmem((ny, rows, feat), BF16),
            vmem((ny, rows, feat), BF16),
            vmem((2, hy, rows, feat), BF16),
            vmem((2, hy, rows, feat), BF16),
            sem((5,)),
            sem((ny - 1,)), sem((ny - 1,)), sem((ny,)), sem((ny,)),
            sem((2, 2, hy)), sem((2, 2, hy)), sem((2, 2 * hy + 1)), sem((2, 2 * hy + 1)),
            sem((experts, 2, hx)), sem((experts, 2, hx)),
            sem((experts, 2, hx)), sem((experts, 2, hx)),
            sem((ny,)), sem((ny,)),
            sem((4, 2, hy)), sem((4, 2, hy)),
        ],
        compiler_params=pltpu.CompilerParams(
            collective_id=0, has_side_effects=True, vmem_limit_bytes=56 * 1024 * 1024
        ),
        name="experts_and_attention",
    )(
        expert_ids.T, gate_weight.T, tokens, lengths, query, w_gate, w_up, w_down,
        cache_k.reshape(seqs, keys, size), cache_v.reshape(seqs, keys, size),
    )
    return (moe, attended.reshape(seqs, heads * size))


def solution(mesh):
    return jax.shard_map(
        body,
        mesh=mesh,
        in_specs=(
            P(("groups", "attn"), "expert"),
            P(("groups", "attn"), None),
            P(("groups", "attn"), None),
            P("attn", "expert", None),
            P("attn", "expert", None),
            P("attn", None, "expert"),
            P(("groups", "attn", "expert"), None, None),
            P(("groups", "attn", "expert"), None, None, None),
            P(("groups", "attn", "expert"), None, None, None),
            P(("groups", "attn", "expert")),
        ),
        out_specs=(P(("groups", "attn"), "expert"), P(("groups", "attn", "expert"), None)),
        check_vma=False,
    )
```

time: 248 us -> 112 us (0.45)
  waiting for transfers between devices: 196 us -> 0 us
  Pallas kernels: 0 us -> 107 us
  matrix products: 14.6 us -> 0 us
  between operations: 13.9 us -> 0.64 us
  other arithmetic: 9.26 us -> 0 us
  local copies, waits for them, and re-layouts: 11.5 us -> 2.97 us
    pallas_call x0 -> x1, Pallas kernels: none -> 107 us  [body(): pl.pallas_call(functools.partial(kernel, ny, nx, kv_heads), out_shape=(ja...]
    reduce_scatter x2 -> x0, waiting for transfers between devices: 99.5 us -> none  [the longest x1 56.3 us: body(): lax.psum_scatter(partial.astype(jnp.bfloat16), 'attn', scatter_dimension=...]
    all_gather x2 -> x0, waiting for transfers between devices: 96.5 us -> none  [the longest x1 60 us: body(): whole = lax.all_gather(block, 'attn', axis=0, tiled=False)]
    dot_general x6 -> x0, matrix products: 14.6 us -> none  [the longest x1 5.92 us: body(): jnp.einsum('tjr,jrd->td', weigh, results, preferred_element_type=jnp.floa...]
    convert_element_type x5 -> x0, local copies, waits for them, and re-layouts: 6.32 us -> none  [the longest x2 3.1 us: body(): whole_gates.astype(jnp.float32)[:, :, None]]
    convert_element_type x4 -> x0, other arithmetic: 3.6 us -> none  [the longest x1 1.06 us: body(): row_sums = lax.psum_scatter(both_parts.astype(jnp.bfloat16), 'expert', sc...]
  transfers between devices with their start and end apart: 4 -> 0, of which waited for: 4 -> 0; matrix products, arithmetic and copies ran while one was open for 4% -> 0% of each run, Pallas kernels for 0% -> 0%
where the time goes in v2:
time: 112 us; the launch traced here: 111 us
  Pallas kernels  107 us (96%)
  local copies, waits for them, and re-layouts  2.97 us (3%)
    pallas_call x1, Pallas kernels, body(): pl.pallas_call(functools.partial(kernel, ny, nx, kv_heads), out_shape=(ja...  107 us
    unnamed x2, local copies, waits for them, and re-layouts  2.97 us

profile of v2, /device:TPU:513, one launch (start us, length us, event | category | flops | bytes accessed | tf_op | source)
XLA Modules:
  0.0 110.6 jit_solution(13772150731998376790)
XLA Ops:
  0.6 106.9 %experts_and_attention.1 = (bf16[128,512]{1,0:T(8,128)(2,1)}, bf16[2,64,128]{2,1,0:T(8,128)(2,1)}) custom-call(s32[8,128]{1,0:T(8,128)} %bitcast.12, bf16[8,128]{1,0:T(8,128)(2,1)} %bitcast.13, bf16[128,512]{1,0:T(8,128)(2,1)} %tok_ref.1, s32[2]{0:T(128)} %len_ref.1, bf16[2,64,128]{2,1,0:T(8,128)(2,1)} %q_ref.1, bf16[4,512,768]{2,1,0:T(8,128)(2,1)} %wg_hbm.1, ...), custom_call_target="tpu_custom_call" | custom-call | tf_op jit(solution)/shard_map/experts_and_attention/pallas_call | solution.py:376
  107.6 1.4 %copy.14 = bf16[1,2,64,128]{3,1,2,0:T(2,128)(2,1)} copy(bf16[1,2,64,128]{3,2,1,0:T(8,128)(2,1)} %bitcast.11) | data formatting | bytes 65536
  109.0 1.6 %copy.16 = bf16[128,512]{1,0:T(8,128)(2,1)} copy(bf16[128,512]{1,0:T(8,128)(2,1)} %get-tuple-element.8) | data formatting | bytes 262144

commit v3 on v2

v3 whole, which is shorter than its diff:
```python
import functools

import jax
import jax.numpy as jnp
from jax import lax
from jax.experimental import pallas as pl
from jax.experimental.pallas import tpu as pltpu
from jax.sharding import PartitionSpec as P

MESH = pl.DeviceIdType.MESH
BF16 = jnp.bfloat16
F32 = jnp.float32
CORES = 2


def dot(a, b):
    return jnp.dot(a, b, preferred_element_type=F32)


def kernel(
    ny, nx, kv_heads,
    ids_hbm, gates_hbm, tok_hbm, len_hbm, q_hbm, wg_hbm, wu_hbm, wd_hbm, k_hbm, v_hbm,
    moe_ref, attn_ref,
    ids_ref, gates_ref, tok_ref, len_ref, q_ref,
    wgu, wd, kbuf, vbuf, tok_all, info_all, memb_s, gate_s, pos_s, pos_t, gate_t, acc, part, rs_buf,
    hid, out_all, weigh, comb, d2_send, d2_recv, y_send, y_recv, moe_s, attn_s,
    load_sem, w_sem, wd_sem, kv_sem, store_sem, out_sem, inf_r, infd_r, ag_r, agd_r, rs_r, hx_r, rd_r, ry_r,
):
    experts, feat, ff = wg_hbm.shape
    rows = tok_ref.shape[0]
    cap = acc.shape[1]
    share = cap // nx
    hy, hx = ny // 2, nx // 2
    blocks = ny * CORES
    seqs = q_hbm.shape[0]
    ai, xi = lax.axis_index("attn"), lax.axis_index("expert")
    y, c = lax.div(ai, CORES), lax.rem(ai, CORES)

    def ring(i, n):
        return lax.rem(i + n, n)

    def at_y(i):
        return {"attn": ring(i, ny) * CORES + c}

    partner = {"attn": y * CORES + (1 - c)}
    y_dev = (at_y(y + 1), at_y(y - 1))
    x_dev = ({"expert": ring(xi + 1, nx)}, {"expert": ring(xi - 1, nx)})
    sign = (1, -1)

    barrier = pltpu.get_barrier_semaphore()
    peers = [*y_dev, partner, *x_dev]
    for dev in peers:
        pl.semaphore_signal(barrier, inc=1, device_id=dev, device_id_type=MESH)

    def send(src, dst, kind, recv_sem, dev):
        copy = pltpu.make_async_remote_copy(
            src_ref=src, dst_ref=dst, send_sem=out_sem.at[kind], recv_sem=recv_sem,
            device_id=dev, device_id_type=MESH,
        )
        copy.start()
        return copy

    def wait_bytes(sem, ref):
        pltpu.make_async_copy(ref, ref, sem).wait()

    def load(src, dst, sem):
        copy = pltpu.make_async_copy(src, dst, sem)
        copy.start()
        return copy

    small = [
        load(tok_hbm, tok_ref, load_sem.at[0]),
        load(ids_hbm, ids_ref, load_sem.at[1]),
        load(gates_hbm, gates_ref, load_sem.at[2]),
    ]
    for copy in small[1:]:
        copy.wait()
    info = jnp.concatenate([ids_ref[...].astype(F32), gates_ref[...].astype(F32)], axis=0).astype(BF16)
    info_all[y, c] = info
    small[0].wait()
    pl.semaphore_wait(barrier, len(peers))

    INFO, PAIR_INFO, AG, PAIR, RS, HD, RD, RY = range(8)
    pieces = 4
    tall = rows // pieces

    def goes(p, d):
        return (p >= pieces // 2) == (d == 1)

    def piece_at(p):
        return pl.ds(p * tall, tall)

    def tok_view(p, yo):
        return tok_all.at[yo, c, piece_at(p)]

    ag, inf = {}, {}

    def ag_send(p, d, s):
        yo = ring(y - sign[d] * (s - 1), ny)
        src = tok_ref.at[piece_at(p)] if s == 1 else tok_view(p, yo)
        ag[p, d, s] = send(src, tok_view(p, yo), AG, ag_r.at[p, d, s - 1], y_dev[d])

    def pair_send(p, d, s):
        yo = ring(y - sign[d] * s, ny)
        src = tok_ref.at[piece_at(p)] if s == 0 else tok_view(p, yo)
        send(src, tok_view(p, yo), PAIR, agd_r.at[s], partner)

    def info_send(d, s):
        view = info_all.at[ring(y - sign[d] * (s - 1), ny), c]
        inf[d, s] = send(view, view, INFO, inf_r.at[d, s - 1], y_dev[d])

    def info_pair(d, s):
        view = info_all.at[ring(y - sign[d] * s, ny), c]
        send(view, view, PAIR_INFO, infd_r.at[0], partner)

    def info_step(s):
        for d in range(2 if s < hy else 1):
            inf[d, s].wait_recv()
            if s + 1 < hy or (s + 1 == hy and d == 0):
                info_send(d, s + 1)
            info_pair(d, s)

    def ag_step(s, p):
        for d in range(2):
            if s == hy and not goes(p, d):
                continue
            ag[p, d, s].wait_recv()
            if s + 1 < hy or (s + 1 == hy and goes(p, d)):
                ag_send(p, d, s + 1)
            pair_send(p, d, s)

    turn = (0, 2, 1, 3)
    for d in range(2):
        info_send(d, 1)
    for p in turn:
        for d in range(2):
            ag_send(p, d, 1)
    info_pair(0, 0)
    for p in range(pieces):
        pair_send(p, 0, 0)
    tok_all[y, c] = tok_ref[...]

    weights = {}

    def load_weights(e):
        weights[e] = (
            load(wg_hbm.at[e], wgu.at[e, :, pl.ds(0, ff)], w_sem.at[0, e]),
            load(wu_hbm.at[e], wgu.at[e, :, pl.ds(ff, ff)], w_sem.at[1, e]),
        )

    def places():
        wait_bytes(infd_r.at[0], info_all.at[:, 0])
        top = ids_ref.shape[0]
        first = ai * experts
        for b in range(blocks):
            both = info_all[b // CORES, b % CORES].astype(F32)
            for e in range(experts):
                equal = both[:top] == (first + e).astype(F32)
                row = e * blocks + b
                memb_s[row : row + 1, :] = jnp.sum(jnp.where(equal, 1.0, 0.0), axis=0, keepdims=True)
                gate_s[row : row + 1, :] = jnp.sum(jnp.where(equal, both[top:], 0.0), axis=0, keepdims=True)
        lines = experts * blocks
        member = memb_s[...]
        iota0 = lax.broadcasted_iota(jnp.int32, (rows, rows), 0)
        iota1 = lax.broadcasted_iota(jnp.int32, (rows, rows), 1)
        before = dot(member.astype(BF16), jnp.where(iota0 < iota1, 1.0, 0.0).astype(BF16))
        counts = dot(member.astype(BF16), jnp.ones((rows, rows), BF16))
        line0 = lax.broadcasted_iota(jnp.int32, (lines, lines), 0)
        line1 = lax.broadcasted_iota(jnp.int32, (lines, lines), 1)
        earlier = (lax.div(line0, blocks) == lax.div(line1, blocks)) & (line1 < line0)
        offset = dot(jnp.where(earlier, 1.0, 0.0).astype(BF16), counts.astype(BF16))
        pos_s[...] = jnp.where(member > 0.5, before + offset, -1.0)

    def turned():
        pad = jnp.zeros((rows - experts * blocks, rows), F32)
        pos_t[...] = jnp.concatenate([pos_s[...], pad], axis=0).T
        gate_t[...] = jnp.concatenate([gate_s[...], pad], axis=0).T

    slot_row = lax.broadcasted_iota(jnp.int32, (cap, rows), 0).astype(F32)

    def dispatch(e, yc):
        picks = []
        for cc in range(CORES):
            line = pos_s[pl.ds(e * blocks + yc * CORES + cc, 1), :]
            picks.append(jnp.where(line == slot_row, 1.0, 0.0))
        pick = jnp.concatenate(picks, axis=1).astype(BF16)
        return dot(pick, tok_all[yc].reshape(CORES * rows, feat))

    def pair_wait(s):
        wait_bytes(agd_r.at[s], tok_all.at[0] if 0 < s < hy else tok_all.at[0, 0])

    def gather_in(s, d):
        if d == 0:
            pair_wait(s)
        for e in range(experts):
            new = dispatch(e, ring(y - sign[d] * s, ny))
            acc[e] = new if s == 0 else acc[e] + new

    info_step(1)
    for n, p in enumerate(turn):
        ag_step(1, p)
    info_step(2)
    for n, p in enumerate(turn):
        ag_step(2, p)
        load_weights(n)
        if n == 1:
            info_step(3)
    ag_step(3, turn[0])
    info_step(4)
    ag_step(3, turn[1])
    places()
    ag_step(3, turn[2])
    gather_in(0, 0)
    ag_step(3, turn[3])
    gather_in(1, 0)
    gather_in(1, 1)
    ag_step(4, turn[0])
    ag_step(4, turn[1])
    gather_in(2, 0)
    ag_step(4, turn[2])
    ag_step(4, turn[3])
    gather_in(2, 1)
    gather_in(3, 0)
    gather_in(3, 1)
    pair_wait(hy)

    rs = {}
    half_share = share // 2

    def rs_send(e, d, s):
        dest = ring(xi + sign[d] * (hx + 1 - s), nx)
        if s == 1:
            at = pl.ds(d * half_share, half_share)
            src, dst = part.at[e, dest, at], rs_buf.at[d, 0, e, at]
        else:
            src, dst = rs_buf.at[d, s - 2, e], rs_buf.at[d, s - 1, e]
        rs[e, d, s] = send(src, dst, RS, rs_r.at[e, d, s - 1], x_dev[d])

    wide = 2 * ff
    step_cols = wide // 3
    for e in range(experts):
        packed = (acc[e] + dispatch(e, ring(y + hy, ny))).astype(BF16)
        for copy in weights[e]:
            copy.wait()
        for n in range(3):
            at = pl.ds(n * step_cols, step_cols)
            part[e, :, :, at] = (
                dot(packed, wgu[e, :, at]).astype(BF16).reshape(nx, share, step_cols)
            )
        for d in range(2):
            rs_send(e, d, 1)

    slot_col = lax.broadcasted_iota(jnp.int32, (rows, cap), 1).astype(F32)

    def weigh_block(b):
        for e in range(experts):
            line = e * blocks + b
            at_col = pos_t[:, line : line + 1]
            gate_col = gate_t[:, line : line + 1]
            weigh[b // CORES, b % CORES, :, e * cap : (e + 1) * cap] = jnp.where(
                at_col == slot_col, gate_col, 0.0
            ).astype(BF16)

    attn_in, stores, down_in = {}, [], {}

    def load_attention(i):
        attn_in[i] = [
            load(k_hbm.at[i], kbuf.at[i], kv_sem.at[i, 0]),
            load(v_hbm.at[i], vbuf.at[i], kv_sem.at[i, 1]),
            load(q_hbm.at[i], q_ref.at[i], kv_sem.at[i, 2]),
        ]
        if i == 0:
            attn_in[i].append(load(len_hbm, len_ref, load_sem.at[3]))

    def attend(i):
        for copy in attn_in[i]:
            copy.wait()
        heads, size = q_ref.shape[1:]
        keys = kbuf.shape[1]
        group = heads // kv_heads
        scores = lax.dot_general(
            q_ref[i], kbuf[i], (((1,), (1,)), ((), ())), preferred_element_type=F32
        ) * size ** (-0.5)
        col = lax.broadcasted_iota(jnp.int32, (heads, keys), 1)
        head = lax.broadcasted_iota(jnp.int32, (heads, keys), 0)
        live = (lax.rem(col, kv_heads) == lax.div(head, group)) & (col < len_ref[i] * kv_heads)
        masked = jnp.where(live, scores, -jnp.inf)
        weighted = jnp.exp(masked - jnp.max(masked, axis=1, keepdims=True))
        total = jnp.sum(weighted, axis=1, keepdims=True)
        prob = (weighted * (1.0 / total)).astype(BF16)
        attn_s[i] = dot(prob, vbuf[i]).astype(BF16)
        stores.append(load(attn_s.at[i], attn_ref.at[i], store_sem.at[i]))

    def load_down(e):
        down_in[e] = load(wd_hbm.at[e], wd.at[e], wd_sem.at[e])

    def settle_early():
        wait_bytes(out_sem.at[INFO], info_all.at[pl.ds(0, ny - 1), 0])
        wait_bytes(out_sem.at[PAIR_INFO], info_all.at[:, 0])
        wait_bytes(out_sem.at[AG], d2_recv.at[pl.ds(0, ny - 1)])
        wait_bytes(out_sem.at[PAIR], d2_recv)

    def weigh_blocks(b):
        weigh_block(b)
        weigh_block(b + 1)

    todo = [turned] + [functools.partial(load_attention, i) for i in range(seqs)]
    todo += [functools.partial(load_down, e) for e in range(experts)]
    todo += [functools.partial(attend, i) for i in range(seqs)]
    todo += [functools.partial(weigh_blocks, b) for b in range(0, blocks, 2)]
    todo += [settle_early]
    for s in range(1, hx):
        for e in range(experts):
            for d in range(2):
                rs[e, d, s].wait_recv()
                dest = ring(xi + sign[d] * (hx - s), nx)
                if s == 1:
                    got, new = pl.ds(d * half_share, half_share), pl.ds((1 - d) * half_share, half_share)
                    rs_buf[d, 0, e, got] = (
                        rs_buf[d, 0, e, got].astype(F32) + part[e, dest, got].astype(F32)
                    ).astype(BF16)
                    rs_buf[d, 0, e, new] = part[e, dest, new]
                else:
                    rs_buf[d, s - 1, e] = (
                        rs_buf[d, s - 1, e].astype(F32) + part[e, dest].astype(F32)
                    ).astype(BF16)
                rs_send(e, d, s + 1)
            for _ in range(1 if s == 1 else 2):
                if todo:
                    todo.pop(0)()
    for job in todo:
        job()

    hd = {}

    def hid_send(e, d, s):
        xo = ring(xi - sign[d] * (s - 1), nx)
        view = hid.at[e, xo]
        if s == hx:
            view = hid.at[e, xo, pl.ds(d * half_share, half_share)]
        hd[e, d, s] = send(view, view, HD, hx_r.at[e, d, s - 1], x_dev[d])

    for e in range(experts):
        for d in range(2):
            rs[e, d, hx].wait_recv()
        total = part[e, xi].astype(F32) + rs_buf[0, hx - 1, e].astype(F32) + rs_buf[1, hx - 1, e].astype(F32)
        gate = total[:, :ff]
        hid[e, xi] = (gate / (1.0 + jnp.exp(-gate)) * total[:, ff:]).astype(BF16)
        for d in range(2):
            hid_send(e, d, 1)
    for s in range(1, hx):
        for e in range(experts):
            for d in range(2):
                hd[e, d, s].wait_recv()
                hid_send(e, d, s + 1)
    wait_bytes(out_sem.at[RS], part.at[:, pl.ds(0, nx - 1)])
    for e in range(experts):
        down_in[e].wait()
        for d in range(2):
            hd[e, d, hx].wait_recv()
        out_all[e * cap : (e + 1) * cap, :] = dot(hid[e].reshape(cap, ff), wd[e]).astype(BF16)

    def slot_of(d, k):
        return 0 if k == 0 else ny - 1 if k == hy else 2 * k - 1 + d

    rd, ry = {}, {}

    def combine(d, k):
        slot = slot_of(d, k)
        yd = ring(y + sign[d] * k, ny)
        both = dot(weigh[yd].reshape(CORES * rows, experts * cap), out_all[...]).reshape(CORES, rows, feat)
        d2_send[slot] = both.astype(BF16)
        rd[slot] = send(d2_send.at[slot, 1 - c], d2_recv.at[slot], RD, rd_r.at[slot], partner)
        comb[slot] = both

    def join(d, k):
        slot = slot_of(d, k)
        rd[slot].wait_recv()
        comb[slot, c] += d2_recv[slot].astype(F32)

    def ry_step(s, long):
        for p in turn:
            for d in range(2):
                if goes(p, d) != long:
                    continue
                at = piece_at(p)
                value = comb[slot_of(d, hy + 1 - s), c, at]
                if s > (1 if long else 2):
                    ry[p, d, s - 1].wait_recv()
                    value = value + y_recv[d, s - 2, at].astype(F32)
                y_send[d, s - 1, at] = value.astype(BF16)
                ry[p, d, s] = send(
                    y_send.at[d, s - 1, at], y_recv.at[d, s - 1, at], RY, ry_r.at[p, d, s - 1], y_dev[d]
                )

    def both_ways(job, k):
        for d in range(2 if 0 < k < hy else 1):
            job(d, k)

    both_ways(combine, hy)
    both_ways(combine, hy - 1)
    both_ways(join, hy)
    ry_step(1, True)
    both_ways(combine, hy - 2)
    both_ways(join, hy - 1)
    ry_step(2, False)
    for k in range(hy - 3, -1, -1):
        both_ways(combine, k)
    both_ways(join, hy - 2)
    ry_step(2, True)
    for s in range(3, hy + 1):
        ry_step(s, False)
        if s < hy:
            both_ways(join, hy - s)
        else:
            join(0, 0)
        ry_step(s, True)
    wait_bytes(out_sem.at[HD], hid.at[:, pl.ds(0, nx - 1)])
    wait_bytes(out_sem.at[RD], d2_recv)
    for p in turn:
        at = piece_at(p)
        value = comb[0, c, at]
        for d in range(2):
            ry[p, d, hy].wait_recv()
            value = value + y_recv[d, hy - 1, at].astype(F32)
        moe_s[at, :] = value.astype(BF16)
        stores.append(load(moe_s.at[at], moe_ref.at[at], store_sem.at[len(stores)]))
    wait_bytes(out_sem.at[RY], d2_recv.at[pl.ds(0, ny - 1)])
    for store in stores:
        store.wait()


def body(tokens, expert_ids, gate_weight, w_gate, w_up, w_down, query, cache_k, cache_v, lengths):
    rows, feat = tokens.shape
    top = expert_ids.shape[1]
    experts, _, ff = w_gate.shape
    attn, nx = lax.axis_size("attn"), lax.axis_size("expert")
    ny = attn // CORES
    cap = rows * top // experts
    share = cap // nx
    seqs, heads, size = query.shape
    context, kv_heads = cache_k.shape[1:3]
    keys = context * kv_heads
    lines = experts * attn
    hy, hx = ny // 2, nx // 2
    vmem = pltpu.VMEM
    sem = pltpu.SemaphoreType.DMA
    in_hbm = pl.BlockSpec(memory_space=pl.ANY)
    moe, attended = pl.pallas_call(
        functools.partial(kernel, ny, nx, kv_heads),
        out_shape=(
            jax.ShapeDtypeStruct((rows, feat), BF16),
            jax.ShapeDtypeStruct((seqs, heads, size), BF16),
        ),
        in_specs=[in_hbm] * 10,
        out_specs=(in_hbm, in_hbm),
        scratch_shapes=[
            vmem((top, rows), jnp.int32),
            vmem((top, rows), BF16),
            vmem((rows, feat), BF16),
            pltpu.SMEM((seqs,), jnp.int32),
            vmem((seqs, heads, size), BF16),
            vmem((experts, feat, 2 * ff), BF16),
            vmem((experts, ff, feat), BF16),
            vmem((seqs, keys, size), BF16),
            vmem((seqs, keys, size), BF16),
            vmem((ny, CORES, rows, feat), BF16),
            vmem((ny, CORES, 2 * top, rows), BF16),
            vmem((lines, rows), F32),
            vmem((lines, rows), F32),
            vmem((lines, rows), F32),
            vmem((rows, rows), F32),
            vmem((rows, rows), F32),
            vmem((experts, cap, feat), F32),
            vmem((experts, nx, share, 2 * ff), BF16),
            vmem((2, hx, experts, share, 2 * ff), BF16),
            vmem((experts, nx, share, ff), BF16),
            vmem((experts * cap, feat), BF16),
            vmem((ny, CORES, rows, experts * cap), BF16),
            vmem((ny, CORES, rows, feat), F32),
            vmem((ny, CORES, rows, feat), BF16),
            vmem((ny, rows, feat), BF16),
            vmem((2, hy, rows, feat), BF16),
            vmem((2, hy, rows, feat), BF16),
            vmem((rows, feat), BF16),
            vmem((seqs, heads, size), BF16),
            sem((4,)), sem((2, experts)), sem((experts,)), sem((seqs, 3)), sem((seqs + 4,)), sem((8,)),
            sem((2, hy)), sem((1,)), sem((4, 2, hy)), sem((hy + 1,)),
            sem((experts, 2, hx)), sem((experts, 2, hx)), sem((ny,)), sem((4, 2, hy)),
        ],
        compiler_params=pltpu.CompilerParams(
            collective_id=0, has_side_effects=True, vmem_limit_bytes=56 * 1024 * 1024
        ),
        name="experts_and_attention",
    )(
        expert_ids.T, gate_weight.T, tokens, lengths, query, w_gate, w_up, w_down,
        cache_k.reshape(seqs, keys, size), cache_v.reshape(seqs, keys, size),
    )
    return (moe, attended.reshape(seqs, heads * size))


def solution(mesh):
    return jax.shard_map(
        body,
        mesh=mesh,
        in_specs=(
            P(("groups", "attn"), "expert"),
            P(("groups", "attn"), None),
            P(("groups", "attn"), None),
            P("attn", "expert", None),
            P("attn", "expert", None),
            P("attn", None, "expert"),
            P(("groups", "attn", "expert"), None, None),
            P(("groups", "attn", "expert"), None, None, None),
            P(("groups", "attn", "expert"), None, None, None),
            P(("groups", "attn", "expert")),
        ),
        out_specs=(P(("groups", "attn"), "expert"), P(("groups", "attn", "expert"), None)),
        check_vma=False,
    )
```

time: 112 us -> 108 us (0.964); the launches traced: 111 us -> 108 us
  Pallas kernels: 107 us -> 104 us
    pallas_call x1, Pallas kernels: 107 us -> 104 us  [body(): pl.pallas_call(functools.partial(kernel, ny, nx, kv_heads), out_shape=(ja...]
where the time goes in v3:
time: 108 us
  Pallas kernels  104 us (96%)
  local copies, waits for them, and re-layouts  2.97 us (3%)
    pallas_call x1, Pallas kernels, body(): pl.pallas_call(functools.partial(kernel, ny, nx, kv_heads), out_shape=(ja...  104 us
    unnamed x2, local copies, waits for them, and re-layouts  2.97 us

profile of v3, /device:TPU:513, one launch (start us, length us, event | category | flops | bytes accessed | tf_op | source)
XLA Modules:
  0.0 107.7 jit_solution(13804958960627749147)
XLA Ops:
  0.6 104.1 %experts_and_attention.1 = (bf16[128,512]{1,0:T(8,128)(2,1)}, bf16[2,64,128]{2,1,0:T(8,128)(2,1)}) custom-call(s32[8,128]{1,0:T(8,128)} %bitcast.12, bf16[8,128]{1,0:T(8,128)(2,1)} %bitcast.13, bf16[128,512]{1,0:T(8,128)(2,1)} %tok_hbm.1, s32[2]{0:T(128)} %len_hbm.1, bf16[2,64,128]{2,1,0:T(8,128)(2,1)} %q_hbm.1, bf16[4,512,768]{2,1,0:T(8,128)(2,1)} %wg_hbm.1, ...), custom_call_target="tpu_custom_call" | custom-call | tf_op jit(solution)/shard_map/experts_and_attention/pallas_call | solution.py:449
  104.7 1.4 %copy.14 = bf16[1,2,64,128]{3,1,2,0:T(2,128)(2,1)} copy(bf16[1,2,64,128]{3,2,1,0:T(8,128)(2,1)} %bitcast.11) | data formatting | bytes 65536
  106.1 1.6 %copy.16 = bf16[128,512]{1,0:T(8,128)(2,1)} copy(bf16[128,512]{1,0:T(8,128)(2,1)} %get-tuple-element.8) | data formatting | bytes 262144
